TPU v7x, 16 devices: a whole 2x2x2 slice. The times are simulated.
16 devices in a mesh: dp: 1, tp: 16 (over x, y, z, core).
Axes of the slice: x: 2, y: 2, z: 2, core: 2. Of those that a mesh axis runs over, the one named last changes fastest.
Arguments:
- x: bfloat16 [2048, 5120], P('dp')
- dy: bfloat16 [2048, 5120], P('dp')
- gate: bfloat16 [2048, 16384], P('dp', 'tp')
- up: bfloat16 [2048, 16384], P('dp', 'tp')
- w_gate: bfloat16 [5120, 16384], P(None, 'tp')
- w_up: bfloat16 [5120, 16384], P(None, 'tp')
- w_down: bfloat16 [16384, 5120], P('tp')
Outputs:
- output 1: bfloat16 [2048, 5120], P('dp')
- output 2: bfloat16 [5120, 16384], P('dp', 'tp')
- output 3: bfloat16 [5120, 16384], P('dp', 'tp')
- output 4: bfloat16 [16384, 5120], P(('dp', 'tp'))
All inputs are finite; a program needn't handle non-finite values.
Results may differ from a plain program's by a relative error of at most 0.012.
Values are sent between devices in bfloat16 or wider.
A program may use at most 2 GiB of HBM per device.

v0:
```python
import jax
import jax.numpy as jnp
from jax import lax
from jax.sharding import PartitionSpec as P


def act(gate, up):
    return jax.nn.silu(gate) * up


def solution(mesh):
    def step(x, dy, gate, up, w_gate, w_up, w_down):
        hidden, back = jax.vjp(act, gate.astype(jnp.float32), up.astype(jnp.float32))
        d_hidden = jnp.dot(dy, w_down.T, preferred_element_type=jnp.float32)
        d_gate, d_up = (g.astype(jnp.bfloat16) for g in back(d_hidden))
        term = jnp.dot(d_gate, w_gate.T, preferred_element_type=jnp.float32) + jnp.dot(d_up, w_up.T, preferred_element_type=jnp.float32)
        dx = lax.psum(term.astype(jnp.bfloat16), "tp")
        dw_gate = jnp.dot(x.T, d_gate, preferred_element_type=jnp.float32)
        dw_up = jnp.dot(x.T, d_up, preferred_element_type=jnp.float32)
        dw_down = jnp.dot(hidden.astype(jnp.bfloat16).T, dy, preferred_element_type=jnp.float32)
        return dx, *(g.astype(jnp.bfloat16) for g in (dw_gate, dw_up, dw_down))

    tokens, columns, rows = P("dp", None), P(None, "tp"), P("tp", None)
    return jax.shard_map(
        step,
        mesh=mesh,
        in_specs=(tokens, tokens, P("dp", "tp"), P("dp", "tp"), columns, columns, rows),
        out_specs=(tokens, P("dp", "tp"), P("dp", "tp"), P(("dp", "tp"), None)),
        check_vma=False,
    )
```

profile of v0, /device:TPU:0, one launch (start us, length us, event | category | flops | bytes accessed | tf_op | source)
XLA Modules:
  0.0 347.6 jit_solution(17292756783557466585)
XLA Ops:
  7.2 0.0 all-reduce.2.cloned.1.call-start
  7.2 32.8 %fusion.6 = (bf16[2048,1024]{1,0:T(8,128)(2,1)}, f32[2048,1024]{1,0:T(8,128)}) fusion(bf16[2048,1024]{1,0:T(8,128)(2,1)} %param.9, bf16[2048,1024]{1,0:T(8,128)(2,1)} %param.10, bf16[2048,5120]{1,0:T(8,128)(2,1)} %param.8, bf16[1024,5120]{1,0:T(8,128)(2,1)} %param.13), kind=kOutput, calls=%fused_computation.16 | convolution fusion | flops 21502099456 | bytes 52428800 | tf_op jit(solution)/shard_map/dot_general | solution.py:14
  40.0 29.6 %fusion.9 = f32[2048,5120]{1,0:T(8,128)} fusion(bf16[2048,1024]{1,0:T(8,128)(2,1)} %get-tuple-element.8, bf16[5120,1024]{1,0:T(8,128)(2,1)} %param.11), kind=kOutput, calls=%fused_computation.19 | convolution fusion | flops 21474836480 | bytes 56623104 | tf_op jit(solution)/shard_map/dot_general | solution.py:16
  69.6 36.8 %add_convert_fusion = bf16[2048,5120]{1,0:T(8,128)(2,1)} fusion(f32[2048,5120]{1,0:T(8,128)} %fusion.9, bf16[5120,1024]{1,0:T(8,128)(2,1)} %param.12, f32[2048,1024]{1,0:T(8,128)} %get-tuple-element.9, bf16[2048,1024]{1,0:T(8,128)(2,1)} %param.9), kind=kOutput, calls=%fused_computation | convolution fusion | flops 21510488064 | bytes 85983232 | tf_op jit(solution)/shard_map/dot_general | solution.py:16
  106.4 0.0 all-reduce.2.cloned.1.call-update
  106.4 28.3 %convert_bitcast_fusion.1 = bf16[5120,1024]{0,1:T(8,128)(2,1)} fusion(bf16[2048,1024]{1,0:T(8,128)(2,1)} %get-tuple-element.8, bf16[2048,5120]{1,0:T(8,128)(2,1)} %param.7), kind=kOutput, calls=%fused_computation.8 | convolution fusion | flops 21480079360 | bytes 35651584 | tf_op jit(solution)/shard_map/dot_general | solution.py:18
  134.7 14.4 %copy.11 = bf16[5120,1024]{1,0:T(8,128)(2,1)} copy(bf16[5120,1024]{0,1:T(8,128)(2,1)} %convert_bitcast_fusion.1) | data formatting | bytes 20971520
  149.1 33.9 %convert_bitcast_fusion = bf16[5120,1024]{0,1:T(8,128)(2,1)} fusion(bf16[2048,5120]{1,0:T(8,128)(2,1)} %param.7, f32[2048,1024]{1,0:T(8,128)} %get-tuple-element.9, bf16[2048,1024]{1,0:T(8,128)(2,1)} %param.9), kind=kOutput, calls=%fused_computation.7 | convolution fusion | flops 21494759424 | bytes 44040192 | tf_op jit(solution)/shard_map/dot_general | solution.py:19
  182.9 14.4 %copy.12 = bf16[5120,1024]{1,0:T(8,128)(2,1)} copy(bf16[5120,1024]{0,1:T(8,128)(2,1)} %convert_bitcast_fusion) | data formatting | bytes 20971520
  197.3 33.2 %convolution_convert_fusion = bf16[1024,5120]{1,0:T(8,128)(2,1)} fusion(bf16[2048,5120]{1,0:T(8,128)(2,1)} %param.8, bf16[2048,1024]{1,0:T(8,128)(2,1)} %param.10, bf16[2048,1024]{1,0:T(8,128)(2,1)} %param.9), kind=kOutput, calls=%fused_computation.9 | convolution fusion | flops 21496856576 | bytes 39845888 | tf_op jit(solution)/shard_map/dot_general | solution.py:20
  230.6 92.8 %all-reduce.2.cloned.1.call-done = bf16[2048,5120]{1,0:T(8,128)(2,1)} async-done(((bf16[2048,5120]{1,0:T(8,128)(2,1)}), bf16[2048,5120]{1,0:T(8,128)(2,1)}) %all-reduce.2.cloned.1.call-update) | async-done | bytes 20971536 | tf_op jit(solution)/shard_map/psum | solution.py:17
  323.4 17.3 %copy.14 = bf16[2048,5120]{1,0:T(8,128)(2,1)} copy(bf16[2048,5120]{1,0:T(8,128)(2,1)} %all-reduce.2.cloned.1.call-done) | data formatting | bytes 41943040
Async XLA Ops:
  7.2 316.3 %all-reduce.2.cloned.1.call-start = ((), (), s32[]{:S(2)}) async-start(), calls=%async_computation | async-start | bytes 41943040 | tf_op jit(solution)/shard_map/psum | solution.py:17
Sparse Core Ops, SparseCore 0:
  106.5 216.8 all-reduce.1
where the time goes:
time: 348 us
  matrix products  195 us (56%)
  waiting for transfers between devices  92.9 us (27%)
  local copies, waits for them, and re-layouts  46.1 us (13%)
  between operations  14 us (4%)
    psum x1, waiting for transfers between devices, step(): dx = lax.psum(term.astype(jnp.bfloat16), 'tp')  92.8 us
    unnamed x3, local copies, waits for them, and re-layouts  46.1 us
    dot_general x1, matrix products, step(): jnp.dot(d_up, w_up.T, preferred_element_type=jnp.float32)  36.8 us
    dot_general x1, matrix products, step(): dw_up = jnp.dot(x.T, d_up, preferred_element_type=jnp.float32)  33.9 us
    dot_general x1, matrix products, step(): jnp.dot(hidden.astype(jnp.bfloat16).T, dy, preferred_element_type=jnp.flo...  33.2 us
    dot_general x1, matrix products, step(): d_hidden = jnp.dot(dy, w_down.T, preferred_element_type=jnp.float32)  32.8 us
    dot_general x1, matrix products, step(): jnp.dot(d_gate, w_gate.T, preferred_element_type=jnp.float32)  29.6 us
    dot_general x1, matrix products, step(): dw_gate = jnp.dot(x.T, d_gate, preferred_element_type=jnp.float32)  28.3 us
  transfers between devices with their start and end apart: 1, of which 1 were waited for; matrix products, arithmetic and copies ran while one was open for 36% of the time, Pallas kernels for 0%

commit v1 on v0

v1 whole, which is shorter than its diff:
```python
import jax
import jax.numpy as jnp
from jax import lax
from jax.experimental import pallas as pl
from jax.experimental.pallas import tpu as pltpu
from jax.sharding import PartitionSpec as P

BF, F32 = jnp.bfloat16, jnp.float32
NT = (((1,), (1,)), ((), ()))
TN = (((0,), (0,)), ((), ()))
MESH = pl.DeviceIdType.MESH

ROWS, D, H = 2048, 5120, 1024
CHUNKS = 4
HALF = ROWS // CHUNKS // 2
Q1, Q2, Q3 = HALF // 2, HALF // 4, HALF // 8
COLS = ((0, 1792), (1792, 1792), (3584, 1536))
TILE = 512
TILES = D // TILE


def dot(a, b, dims):
    return lax.dot_general(a, b, dims, preferred_element_type=F32)


def kernel(x, dy, gate, up, w_gate, w_up, w_down, dx, dwg, dwu, dwd, dg_o, du_o, hd_o,
           acc1, acc2, acc3, ds_, dr, s1, r1, s2, r2, s3, r3, fin,
           d_s, d_r, p1_s, p1_r, p2_s, p2_r, p3_s, p3_r, loc_s,
           a1_s, a1_r, a2_s, a2_r, a3_s, a3_r, dd_s, dd_r):
    me, dp = lax.axis_index("tp"), lax.axis_index("dp")
    core, bz, by, bx = me % 2, me // 2 % 2, me // 4 % 2, me // 8 % 2
    other = me + 1 - 2 * core
    axes = {"x": (bx, me + 8 - 16 * bx), "y": (by, me + 4 - 8 * by), "z": (bz, me + 2 - 4 * bz)}
    orders = [[axes[a] for a in o] for o in ("xyz", "yzx", "zxy")]

    barrier = pltpu.get_barrier_semaphore()
    for peer in (other, axes["x"][1], axes["y"][1], axes["z"][1]):
        pl.semaphore_signal(barrier, inc=1, device_id=(dp, peer), device_id_type=MESH)
    pl.semaphore_wait(barrier, 4)

    def remote(src, dst, ss, rs, peer):
        return pltpu.make_async_remote_copy(src_ref=src, dst_ref=dst, send_sem=ss, recv_sem=rs,
                                            device_id=(dp, peer), device_id_type=MESH)

    def cols(j):
        return pl.ds(*COLS[j])

    def al(v, n):
        return pl.multiple_of(v, n)

    def base(c):
        return c * (2 * HALF) + HALF * core

    def d_copy(c, j):
        return remote(ds_.at[:, cols(j)], dr.at[c % 2, :, cols(j)], d_s.at[j], d_r.at[c % 2, j], other)

    def p1(c, j):
        return remote(s1.at[:, cols(j)], r1.at[c % 2, :, cols(j)], p1_s.at[j], p1_r.at[c % 2, j], orders[j][0][1])

    def p2(c, j):
        return remote(s2.at[c % 2, :, cols(j)], r2.at[c % 2, :, cols(j)], p2_s.at[c % 2, j], p2_r.at[c % 2, j], orders[j][1][1])

    def p3(c, j):
        return remote(s3.at[c % 2, :, cols(j)], r3.at[c % 2, :, cols(j)], p3_s.at[c % 2, j], p3_r.at[c % 2, j], orders[j][2][1])

    def rows3(c, j):
        b = orders[j]
        return pl.ds(al(base(c) + Q1 * b[0][0] + Q2 * b[1][0] + Q3 * b[2][0], Q3), Q3)

    def rows2(c, j):
        b = orders[j]
        return pl.ds(al(base(c) + Q1 * b[0][0] + Q2 * b[1][0], Q2), Q2)

    def rows1(c, j):
        return pl.ds(al(base(c) + Q1 * orders[j][0][0], Q1), Q1)

    def rows0(c):
        return pl.ds(al(base(c), HALF), HALF)

    def loc(c, j):
        return pltpu.make_async_copy(fin.at[c % 2, :, cols(j)], dx.at[rows3(c, j), cols(j)], loc_s.at[c % 2, j])

    def a1(c, j):
        return remote(fin.at[c % 2, :, cols(j)], dx.at[rows3(c, j), cols(j)], a1_s.at[c, j], a1_r.at[c, j], orders[j][2][1])

    def a2(c, j):
        r = dx.at[rows2(c, j), cols(j)]
        return remote(r, r, a2_s.at[c, j], a2_r.at[c, j], orders[j][1][1])

    def a3(c, j):
        r = dx.at[rows1(c, j), cols(j)]
        return remote(r, r, a3_s.at[c, j], a3_r.at[c, j], orders[j][0][1])

    def dd(c, j):
        r = dx.at[rows0(c), cols(j)]
        return remote(r, r, dd_s.at[c, j], dd_r.at[c, j], other)

    def stage1(c):
        for j in range(3):
            bit = orders[j][1][0]
            keep, send = pl.ds(al(Q2 * bit, Q2), Q2), pl.ds(al(Q2 - Q2 * bit, Q2), Q2)
            p1(c, j).wait_recv()

            @pl.when(c >= 2)
            def _():
                p2(c, j).wait_send()
            s2[c % 2, :, cols(j)] = (acc1[send, cols(j)] + r1[c % 2, send, cols(j)].astype(F32)).astype(BF)
            p2(c, j).start()
            acc2[:, cols(j)] = acc1[keep, cols(j)] + r1[c % 2, keep, cols(j)].astype(F32)

    def stage2(c):
        for j in range(3):
            bit = orders[j][2][0]
            keep, send = pl.ds(al(Q3 * bit, Q3), Q3), pl.ds(al(Q3 - Q3 * bit, Q3), Q3)
            p2(c, j).wait_recv()

            @pl.when(c >= 2)
            def _():
                p3(c, j).wait_send()
            s3[c % 2, :, cols(j)] = (acc2[send, cols(j)] + r2[c % 2, send, cols(j)].astype(F32)).astype(BF)
            p3(c, j).start()
            acc3[:, cols(j)] = acc2[keep, cols(j)] + r2[c % 2, keep, cols(j)].astype(F32)

    def stage3(c):
        for j in range(3):
            p3(c, j).wait_recv()

            @pl.when(c >= 2)
            def _():
                a1(c - 2, j).wait_send()
            fin[c % 2, :, cols(j)] = (acc3[:, cols(j)] + r3[c % 2, :, cols(j)].astype(F32)).astype(BF)
            a1(c, j).start()
            loc(c, j).start()

    def stage4(c):
        for j in range(3):
            loc(c, j).wait()
            a1(c, j).wait_recv()
            a2(c, j).start()

    def stage5(c):
        for j in range(3):
            a2(c, j).wait_recv()
            a3(c, j).start()

    def stage6(c):
        for j in range(3):
            a3(c, j).wait_recv()
            dd(c, j).start()

    def stage7(c):
        for j in range(3):
            dd(c, j).wait_recv()

    stages = (None, stage1, stage2, stage3, stage4, stage5, stage6, stage7)

    def terms_phase(wg, wu, wd, dyb, gb, ub, dgb, dub, hdb, ld_w, ld_wd, ld, wr):
        def start_rows(c, h):
            return c * (2 * HALF) + HALF * (core if h else 1 - core)

        def loads(c, h):
            r = pl.ds(al(start_rows(c, h), HALF), HALF)
            return [pltpu.make_async_copy(src.at[r], dst.at[h], ld.at[h, i])
                    for i, (src, dst) in enumerate(((dy, dyb), (gate, gb), (up, ub)))]

        def writes(c, h):
            r = pl.ds(al(start_rows(c, h), HALF), HALF)
            return [pltpu.make_async_copy(src.at[h], dst.at[r], wr.at[h, i])
                    for i, (src, dst) in enumerate(((dgb, dg_o), (dub, du_o), (hdb, hd_o)))]

        def weights(j):
            return [pltpu.make_async_copy(src.at[cols(j)], dst.at[cols(j)], ld_w.at[i, j])
                    for i, (src, dst) in enumerate(((w_gate, wg), (w_up, wu)))]

        for d in loads(0, 0):
            d.start()
        wd_load = pltpu.make_async_copy(w_down, wd, ld_wd)
        wd_load.start()
        for j in range(3):
            for d in weights(j):
                d.start()
        for d in loads(0, 1):
            d.start()
        wd_load.wait()

        def hidden_rows(c, h):
            for d in loads(c, h):
                d.wait()

            @pl.when(c >= 1)
            def _():
                for d in writes(c - 1, h):
                    d.wait()
            g, u = gb[h].astype(F32), ub[h].astype(F32)
            sig = jax.nn.sigmoid(g)
            silu = g * sig
            hdb[h] = (silu * u).astype(BF)
            dh = dot(dyb[h], wd[...], NT)
            dub[h] = (dh * silu).astype(BF)
            dgb[h] = (dh * u * (sig + silu * (1 - sig))).astype(BF)
            for d in writes(c, h):
                d.start()

            @pl.when(c + 1 < CHUNKS)
            def _():
                for d in loads(c + 1, h):
                    d.start()

        def term(h, j):
            return dot(dgb[h], wg[cols(j), :], NT) + dot(dub[h], wu[cols(j), :], NT)

        def chunk(c, carry):
            hidden_rows(c, 0)
            for j in range(3):
                @pl.when(c == 0)
                def _():
                    for d in weights(j):
                        d.wait()

                @pl.when(c >= 1)
                def _():
                    d_copy(c - 1, j).wait_send()
                ds_[:, cols(j)] = term(0, j).astype(BF)
                d_copy(c, j).start()

            @pl.when(c >= 2)
            def _():
                stage2(c - 2)
            hidden_rows(c, 1)

            @pl.when(c >= 1)
            def _():
                stage1(c - 1)

            @pl.when(c >= 3)
            def _():
                stage4(c - 3)
            for j in range(3):
                d_copy(c, j).wait_recv()

                @pl.when(c >= 1)
                def _():
                    p1(c - 1, j).wait_send()
                t = term(1, j) + dr[c % 2, :, cols(j)].astype(F32)
                high = orders[j][0][0] == 1
                s1[:, cols(j)] = jnp.where(high, t[:Q1], t[Q1:]).astype(BF)
                p1(c, j).start()
                acc1[:, cols(j)] = jnp.where(high, t[Q1:], t[:Q1])

            @pl.when(c >= 2)
            def _():
                stage3(c - 2)

            @pl.when(c >= 3)
            def _():
                stage5(c - 3)
            return carry

        lax.fori_loop(0, CHUNKS, chunk, 0)
        for h in range(2):
            for d in writes(CHUNKS - 1, h):
                d.wait()
        for j in range(3):
            d_copy(CHUNKS - 1, j).wait_send()

    bf = lambda *s: pltpu.VMEM(s, BF)
    dma = lambda *s: pltpu.SemaphoreType.DMA(s)
    pl.run_scoped(terms_phase, bf(D, H), bf(D, H), bf(H, D), bf(2, HALF, D), bf(2, HALF, H), bf(2, HALF, H),
                  bf(2, HALF, H), bf(2, HALF, H), bf(2, HALF, H), dma(2, 3), dma(), dma(2, 3), dma(2, 3))

    plan = {(0, 0): [(2, 2)], (1, 0): [(4, 1)], (1, 1): [(1, 3), (3, 2), (5, 1)], (2, 0): [(6, 0)],
            (2, 1): [(2, 3), (4, 2)], (3, 1): [(3, 3), (5, 2)], (4, 0): [(6, 1)], (4, 1): [(4, 3)],
            (5, 1): [(5, 3)], (6, 1): [(6, 2)], (8, 1): [(6, 3)]}

    def weights_phase(dg, du, hd, xb, yb, og, ou, od, ld_f, ld_x, ld_y, wr):
        def tile(t):
            return pl.ds(al(t * TILE, TILE), TILE)

        def load_x(t):
            return pltpu.make_async_copy(x.at[:, tile(t)], xb.at[t % 2], ld_x.at[t % 2])

        def load_y(t):
            return pltpu.make_async_copy(dy.at[:, tile(t)], yb.at[t % 2], ld_y.at[t % 2])

        full = [pltpu.make_async_copy(src, dst, ld_f.at[i])
                for i, (src, dst) in enumerate(((dg_o, dg), (du_o, du), (hd_o, hd)))]

        def writes(t):
            s = t % 2
            return [pltpu.make_async_copy(og.at[s], dwg.at[tile(t)], wr.at[s, 0]),
                    pltpu.make_async_copy(ou.at[s], dwu.at[tile(t)], wr.at[s, 1]),
                    pltpu.make_async_copy(od.at[s], dwd.at[:, tile(t)], wr.at[s, 2])]

        full[0].start()
        load_x(0).start()
        full[1].start()
        full[2].start()
        load_y(0).start()

        def unit(t, carry):
            s = t % 2

            @pl.when(t + 1 < TILES)
            def _():
                load_x(t + 1).start()
                load_y(t + 1).start()

            @pl.when(t >= 2)
            def _():
                for d in writes(t - 2):
                    d.wait()

            def serve(sub):
                for (tt, ss), todo in plan.items():
                    if ss == sub:
                        @pl.when(t == tt)
                        def _():
                            for k, c in todo:
                                stages[k](c)

            @pl.when(t == 0)
            def _():
                full[0].wait()
            load_x(t).wait()
            og[s] = dot(xb[s], dg[...], TN).astype(BF)
            writes(t)[0].start()

            @pl.when(t == 0)
            def _():
                full[1].wait()
            ou[s] = dot(xb[s], du[...], TN).astype(BF)
            writes(t)[1].start()
            serve(0)

            @pl.when(t == 0)
            def _():
                full[2].wait()
            load_y(t).wait()
            od[s] = dot(hd[...], yb[s], TN).astype(BF)
            writes(t)[2].start()
            serve(1)
            return carry

        lax.fori_loop(0, TILES, unit, 0)
        for t in (TILES - 2, TILES - 1):
            for d in writes(t):
                d.wait()

    pl.run_scoped(weights_phase, bf(ROWS, H), bf(ROWS, H), bf(ROWS, H), bf(2, ROWS, TILE), bf(2, ROWS, TILE),
                  bf(2, TILE, H), bf(2, TILE, H), bf(2, H, TILE), dma(3), dma(2), dma(2), dma(2, 3))

    for c in range(CHUNKS):
        stage7(c)
    for j in range(3):
        p1(CHUNKS - 1, j).wait_send()
        for c in (CHUNKS - 2, CHUNKS - 1):
            p2(c, j).wait_send()
            p3(c, j).wait_send()
            a1(c, j).wait_send()
        for c in range(CHUNKS):
            a2(c, j).wait_send()
            a3(c, j).wait_send()
            dd(c, j).wait_send()


def solution(mesh):
    bf = lambda *s: pltpu.VMEM(s, BF)
    dma = lambda *s: pltpu.SemaphoreType.DMA(s)

    def step(x, dy, gate, up, w_gate, w_up, w_down):
        outs = [(ROWS, D), (D, H), (D, H), (H, D), (ROWS, H), (ROWS, H), (ROWS, H)]
        scratch = [pltpu.VMEM((Q1, D), F32), pltpu.VMEM((Q2, D), F32), pltpu.VMEM((Q3, D), F32),
                   bf(HALF, D), bf(2, HALF, D), bf(Q1, D), bf(2, Q1, D), bf(2, Q2, D), bf(2, Q2, D),
                   bf(2, Q3, D), bf(2, Q3, D), bf(2, Q3, D),
                   dma(3), dma(2, 3), dma(3), dma(2, 3), dma(2, 3), dma(2, 3), dma(2, 3), dma(2, 3), dma(2, 3)]
        scratch += [dma(CHUNKS, 3)] * 8
        res = pl.pallas_call(
            kernel,
            in_specs=[pl.BlockSpec(memory_space=pl.ANY)] * 7,
            out_specs=[pl.BlockSpec(memory_space=pl.ANY)] * 7,
            out_shape=[jax.ShapeDtypeStruct(s, BF) for s in outs],
            scratch_shapes=scratch,
            compiler_params=pltpu.CompilerParams(collective_id=0, has_side_effects=True, vmem_limit_bytes=67043328),
        )(x, dy, gate, up, w_gate, w_up, w_down)
        return tuple(res[:4])

    tokens, columns, rows = P("dp", None), P(None, "tp"), P("tp", None)
    return jax.shard_map(
        step,
        mesh=mesh,
        in_specs=(tokens, tokens, P("dp", "tp"), P("dp", "tp"), columns, columns, rows),
        out_specs=(tokens, P("dp", "tp"), P("dp", "tp"), P(("dp", "tp"), None)),
        check_vma=False,
    )
```

time: 348 us -> 241 us (0.69)
  Pallas kernels: 0 us -> 196 us
  matrix products: 195 us -> 0 us
  waiting for transfers between devices: 92.9 us -> 0 us
  between operations: 14 us -> 0.64 us
    pallas_call x0 -> x1, Pallas kernels: none -> 196 us  [step(): pl.pallas_call(kernel, in_specs=[pl.BlockSpec(memory_space=pl.ANY)] * 7,...]
    dot_general x6 -> x0, matrix products: 195 us -> none  [the longest x1 36.8 us: step(): jnp.dot(d_up, w_up.T, preferred_element_type=jnp.float32)]
    psum x1 -> x0, waiting for transfers between devices: 92.8 us -> none  [step(): dx = lax.psum(term.astype(jnp.bfloat16), 'tp')]
    unnamed x3 -> x4, local copies, waits for them, and re-layouts: 46.1 us -> 44.7 us
  transfers between devices with their start and end apart: 1 -> 0, of which waited for: 1 -> 0; matrix products, arithmetic and copies ran while one was open for 36% -> 0% of each run, Pallas kernels for 0% -> 0%
where the time goes in v1:
time: 241 us
  Pallas kernels  196 us (81%)
  local copies, waits for them, and re-layouts  44.7 us (19%)
    pallas_call x1, Pallas kernels, step(): pl.pallas_call(kernel, in_specs=[pl.BlockSpec(memory_space=pl.ANY)] * 7,...  196 us
    unnamed x4, local copies, waits for them, and re-layouts  44.7 us

profile of v1, /device:TPU:0, one launch (start us, length us, event | category | flops | bytes accessed | tf_op | source)
XLA Modules:
  0.0 241.1 jit_solution(16327541321185948280)
XLA Ops:
  0.6 195.8 %shard_map.102 = (bf16[2048,5120]{1,0:T(8,128)(2,1)}, bf16[5120,1024]{1,0:T(8,128)(2,1)}, bf16[5120,1024]{1,0:T(8,128)(2,1)}, bf16[1024,5120]{1,0:T(8,128)(2,1)}...) custom-call(bf16[2048,5120]{1,0:T(8,128)(2,1)} %x.1, bf16[2048,5120]{1,0:T(8,128)(2,1)} %dy.1, ...), custom_call_target="tpu_custom_call" | custom-call | tf_op jit(solution)/shard_map/pallas_call | solution.py:377
  196.4 17.3 %copy.15 = bf16[2048,5120]{1,0:T(8,128)(2,1)} copy(bf16[2048,5120]{1,0:T(8,128)(2,1)} %get-tuple-element.16) | data formatting | bytes 41943040
  213.7 9.3 %copy.16 = bf16[5120,1024]{1,0:T(8,128)(2,1)} copy(bf16[5120,1024]{1,0:T(8,128)(2,1)} %get-tuple-element.17) | data formatting | bytes 20971520
  223.0 9.3 %copy.17 = bf16[5120,1024]{1,0:T(8,128)(2,1)} copy(bf16[5120,1024]{1,0:T(8,128)(2,1)} %get-tuple-element.18) | data formatting | bytes 20971520
  232.3 8.8 %copy.18 = bf16[1024,5120]{1,0:T(8,128)(2,1)} copy(bf16[1024,5120]{1,0:T(8,128)(2,1)} %get-tuple-element.19) | data formatting | bytes 20971520

commit v2 on v1

--- a/solution.py
+++ b/solution.py
@@ -1,3 +1,5 @@
+import functools
+
 import jax
 import jax.numpy as jnp
 from jax import lax
@@ -17,6 +19,13 @@
 COLS = ((0, 1792), (1792, 1792), (3584, 1536))
 TILE = 512
 TILES = D // TILE
+
+PLAN1 = {12: [100, 101, 102], 16: [200, 201, 202], 20: [110, 111, 112], 21: [300, 302], 24: [210, 212], 25: [301, 211], 27: [400], 28: [120, 122,
+         121], 30: [310]}
+PLAN2 = {0: [311, 221, 220], 2: [312, 222, 401, 130, 402], 3: [132], 4: [131], 5: [321], 6: [320, 322, 410, 412], 7: [411], 8: [230, 231, 232], 9:
+         [420, 422], 10: [421], 11: [331, 501], 12: [330, 500], 13: [502], 15: [332], 16: [430, 431, 510], 18: [511, 512, 601], 19: [600, 602], 20:
+         [432], 22: [520, 522], 23: [521, 610], 25: [611, 612], 26: [530, 532], 27: [531], 29: [620, 622]}
+PLAN3 = [621, 632, 630, 631]
 
 
 def dot(a, b, dims):
@@ -36,7 +45,6 @@
     barrier = pltpu.get_barrier_semaphore()
     for peer in (other, axes["x"][1], axes["y"][1], axes["z"][1]):
         pl.semaphore_signal(barrier, inc=1, device_id=(dp, peer), device_id_type=MESH)
-    pl.semaphore_wait(barrier, 4)
 
     def remote(src, dst, ss, rs, peer):
         return pltpu.make_async_remote_copy(src_ref=src, dst_ref=dst, send_sem=ss, recv_sem=rs,
@@ -95,64 +103,57 @@
         r = dx.at[rows0(c), cols(j)]
         return remote(r, r, dd_s.at[c, j], dd_r.at[c, j], other)
 
-    def stage1(c):
-        for j in range(3):
-            bit = orders[j][1][0]
-            keep, send = pl.ds(al(Q2 * bit, Q2), Q2), pl.ds(al(Q2 - Q2 * bit, Q2), Q2)
-            p1(c, j).wait_recv()
-
-            @pl.when(c >= 2)
-            def _():
-                p2(c, j).wait_send()
-            s2[c % 2, :, cols(j)] = (acc1[send, cols(j)] + r1[c % 2, send, cols(j)].astype(F32)).astype(BF)
-            p2(c, j).start()
-            acc2[:, cols(j)] = acc1[keep, cols(j)] + r1[c % 2, keep, cols(j)].astype(F32)
-
-    def stage2(c):
-        for j in range(3):
-            bit = orders[j][2][0]
-            keep, send = pl.ds(al(Q3 * bit, Q3), Q3), pl.ds(al(Q3 - Q3 * bit, Q3), Q3)
-            p2(c, j).wait_recv()
-
-            @pl.when(c >= 2)
-            def _():
-                p3(c, j).wait_send()
-            s3[c % 2, :, cols(j)] = (acc2[send, cols(j)] + r2[c % 2, send, cols(j)].astype(F32)).astype(BF)
-            p3(c, j).start()
-            acc3[:, cols(j)] = acc2[keep, cols(j)] + r2[c % 2, keep, cols(j)].astype(F32)
-
-    def stage3(c):
-        for j in range(3):
-            p3(c, j).wait_recv()
-
-            @pl.when(c >= 2)
-            def _():
-                a1(c - 2, j).wait_send()
-            fin[c % 2, :, cols(j)] = (acc3[:, cols(j)] + r3[c % 2, :, cols(j)].astype(F32)).astype(BF)
-            a1(c, j).start()
-            loc(c, j).start()
-
-    def stage4(c):
-        for j in range(3):
-            loc(c, j).wait()
-            a1(c, j).wait_recv()
-            a2(c, j).start()
-
-    def stage5(c):
-        for j in range(3):
-            a2(c, j).wait_recv()
-            a3(c, j).start()
-
-    def stage6(c):
-        for j in range(3):
-            a3(c, j).wait_recv()
-            dd(c, j).start()
-
-    def stage7(c):
-        for j in range(3):
-            dd(c, j).wait_recv()
-
-    stages = (None, stage1, stage2, stage3, stage4, stage5, stage6, stage7)
+    def stage1(c, j):
+        bit = orders[j][1][0]
+        keep, send = pl.ds(al(Q2 * bit, Q2), Q2), pl.ds(al(Q2 - Q2 * bit, Q2), Q2)
+        p1(c, j).wait_recv()
+        if c >= 2:
+            p2(c - 2, j).wait_send()
+        s2[c % 2, :, cols(j)] = (acc1[send, cols(j)] + r1[c % 2, send, cols(j)].astype(F32)).astype(BF)
+        p2(c, j).start()
+        acc2[:, cols(j)] = acc1[keep, cols(j)] + r1[c % 2, keep, cols(j)].astype(F32)
+
+    def stage2(c, j):
+        bit = orders[j][2][0]
+        keep, send = pl.ds(al(Q3 * bit, Q3), Q3), pl.ds(al(Q3 - Q3 * bit, Q3), Q3)
+        p2(c, j).wait_recv()
+        if c >= 2:
+            p3(c - 2, j).wait_send()
+        s3[c % 2, :, cols(j)] = (acc2[send, cols(j)] + r2[c % 2, send, cols(j)].astype(F32)).astype(BF)
+        p3(c, j).start()
+        acc3[:, cols(j)] = acc2[keep, cols(j)] + r2[c % 2, keep, cols(j)].astype(F32)
+
+    def stage3(c, j):
+        p3(c, j).wait_recv()
+        if c >= 2:
+            a1(c - 2, j).wait_send()
+        fin[c % 2, :, cols(j)] = (acc3[:, cols(j)] + r3[c % 2, :, cols(j)].astype(F32)).astype(BF)
+        a1(c, j).start()
+        loc(c, j).start()
+
+    def stage4(c, j):
+        a1(c, j).wait_recv()
+        loc(c, j).wait()
+        a2(c, j).start()
+
+    def stage5(c, j):
+        a2(c, j).wait_recv()
+        a3(c, j).start()
+
+    def stage6(c, j):
+        a3(c, j).wait_recv()
+        dd(c, j).start()
+
+    stages = (None, stage1, stage2, stage3, stage4, stage5, stage6)
+
+    def run(codes):
+        for code in codes:
+            stages[code // 100](code // 10 % 10, code % 10)
+
+    def serve(plan, per_step, step, sub):
+        for at, codes in plan.items():
+            if at % per_step == sub:
+                pl.when(step == at // per_step)(functools.partial(run, codes))
 
     def terms_phase(wg, wu, wd, dyb, gb, ub, dgb, dub, hdb, ld_w, ld_wd, ld, wr):
         def start_rows(c, h):
@@ -172,16 +173,14 @@
             return [pltpu.make_async_copy(src.at[cols(j)], dst.at[cols(j)], ld_w.at[i, j])
                     for i, (src, dst) in enumerate(((w_gate, wg), (w_up, wu)))]
 
-        for d in loads(0, 0):
+        halves = [pltpu.make_async_copy(w_down.at[pl.ds(i * (H // 2), H // 2)], wd.at[pl.ds(i * (H // 2), H // 2)], ld_wd.at[i])
+                  for i in range(2)]
+        for d in loads(0, 0) + halves:
             d.start()
-        wd_load = pltpu.make_async_copy(w_down, wd, ld_wd)
-        wd_load.start()
-        for j in range(3):
-            for d in weights(j):
-                d.start()
-        for d in loads(0, 1):
+        pl.semaphore_wait(barrier, 4)
+        halves[0].wait()
+        for d in weights(0):
             d.start()
-        wd_load.wait()
 
         def hidden_rows(c, h):
             for d in loads(c, h):
@@ -191,13 +190,21 @@
             def _():
                 for d in writes(c - 1, h):
                     d.wait()
-            g, u = gb[h].astype(F32), ub[h].astype(F32)
-            sig = jax.nn.sigmoid(g)
-            silu = g * sig
-            hdb[h] = (silu * u).astype(BF)
-            dh = dot(dyb[h], wd[...], NT)
-            dub[h] = (dh * silu).astype(BF)
-            dgb[h] = (dh * u * (sig + silu * (1 - sig))).astype(BF)
+            for i in range(2):
+                part = pl.ds(i * (H // 2), H // 2)
+                if h == 0 and i == 1:
+                    @pl.when(c == 0)
+                    def _():
+                        halves[1].wait()
+                        for d in loads(0, 1) + weights(1) + weights(2):
+                            d.start()
+                g, u = gb[h, :, part].astype(F32), ub[h, :, part].astype(F32)
+                sig = jax.nn.sigmoid(g)
+                silu = g * sig
+                hdb[h, :, part] = (silu * u).astype(BF)
+                dh = dot(dyb[h], wd[part, :], NT)
+                dub[h, :, part] = (dh * silu).astype(BF)
+                dgb[h, :, part] = (dh * u * (sig + silu * (1 - sig))).astype(BF)
             for d in writes(c, h):
                 d.start()
 
@@ -211,6 +218,7 @@
 
         def chunk(c, carry):
             hidden_rows(c, 0)
+            serve(PLAN1, 8, c, 0)
             for j in range(3):
                 @pl.when(c == 0)
                 def _():
@@ -222,19 +230,9 @@
                     d_copy(c - 1, j).wait_send()
                 ds_[:, cols(j)] = term(0, j).astype(BF)
                 d_copy(c, j).start()
-
-            @pl.when(c >= 2)
-            def _():
-                stage2(c - 2)
+                serve(PLAN1, 8, c, 1 + j)
             hidden_rows(c, 1)
-
-            @pl.when(c >= 1)
-            def _():
-                stage1(c - 1)
-
-            @pl.when(c >= 3)
-            def _():
-                stage4(c - 3)
+            serve(PLAN1, 8, c, 4)
             for j in range(3):
                 d_copy(c, j).wait_recv()
 
@@ -246,14 +244,7 @@
                 s1[:, cols(j)] = jnp.where(high, t[:Q1], t[Q1:]).astype(BF)
                 p1(c, j).start()
                 acc1[:, cols(j)] = jnp.where(high, t[Q1:], t[:Q1])
-
-            @pl.when(c >= 2)
-            def _():
-                stage3(c - 2)
-
-            @pl.when(c >= 3)
-            def _():
-                stage5(c - 3)
+                serve(PLAN1, 8, c, 5 + j)
             return carry
 
         lax.fori_loop(0, CHUNKS, chunk, 0)
@@ -266,11 +257,7 @@
     bf = lambda *s: pltpu.VMEM(s, BF)
     dma = lambda *s: pltpu.SemaphoreType.DMA(s)
     pl.run_scoped(terms_phase, bf(D, H), bf(D, H), bf(H, D), bf(2, HALF, D), bf(2, HALF, H), bf(2, HALF, H),
-                  bf(2, HALF, H), bf(2, HALF, H), bf(2, HALF, H), dma(2, 3), dma(), dma(2, 3), dma(2, 3))
-
-    plan = {(0, 0): [(2, 2)], (1, 0): [(4, 1)], (1, 1): [(1, 3), (3, 2), (5, 1)], (2, 0): [(6, 0)],
-            (2, 1): [(2, 3), (4, 2)], (3, 1): [(3, 3), (5, 2)], (4, 0): [(6, 1)], (4, 1): [(4, 3)],
-            (5, 1): [(5, 3)], (6, 1): [(6, 2)], (8, 1): [(6, 3)]}
+                  bf(2, HALF, H), bf(2, HALF, H), bf(2, HALF, H), dma(2, 3), dma(2), dma(2, 3), dma(2, 3))
 
     def weights_phase(dg, du, hd, xb, yb, og, ou, od, ld_f, ld_x, ld_y, wr):
         def tile(t):
@@ -285,11 +272,12 @@
         full = [pltpu.make_async_copy(src, dst, ld_f.at[i])
                 for i, (src, dst) in enumerate(((dg_o, dg), (du_o, du), (hd_o, hd)))]
 
-        def writes(t):
+        def write(t, i):
             s = t % 2
-            return [pltpu.make_async_copy(og.at[s], dwg.at[tile(t)], wr.at[s, 0]),
-                    pltpu.make_async_copy(ou.at[s], dwu.at[tile(t)], wr.at[s, 1]),
-                    pltpu.make_async_copy(od.at[s], dwd.at[:, tile(t)], wr.at[s, 2])]
+            if i == 2:
+                return pltpu.make_async_copy(od.at[s], dwd.at[:, tile(t)], wr.at[s, 2])
+            src, dst = ((og, dwg), (ou, dwu))[i]
+            return pltpu.make_async_copy(src.at[s], dst.at[tile(t)], wr.at[s, i])
 
         full[0].start()
         load_x(0).start()
@@ -307,51 +295,36 @@
 
             @pl.when(t >= 2)
             def _():
-                for d in writes(t - 2):
-                    d.wait()
-
-            def serve(sub):
-                for (tt, ss), todo in plan.items():
-                    if ss == sub:
-                        @pl.when(t == tt)
-                        def _():
-                            for k, c in todo:
-                                stages[k](c)
-
-            @pl.when(t == 0)
-            def _():
-                full[0].wait()
-            load_x(t).wait()
-            og[s] = dot(xb[s], dg[...], TN).astype(BF)
-            writes(t)[0].start()
-
-            @pl.when(t == 0)
-            def _():
-                full[1].wait()
-            ou[s] = dot(xb[s], du[...], TN).astype(BF)
-            writes(t)[1].start()
-            serve(0)
-
-            @pl.when(t == 0)
-            def _():
-                full[2].wait()
-            load_y(t).wait()
-            od[s] = dot(hd[...], yb[s], TN).astype(BF)
-            writes(t)[2].start()
-            serve(1)
+                for i in range(3):
+                    write(t - 2, i).wait()
+
+            for i, (out, full_v) in enumerate(((og, dg), (ou, du), (od, hd))):
+                @pl.when(t == 0)
+                def _():
+                    full[i].wait()
+                if i == 0:
+                    load_x(t).wait()
+                if i == 2:
+                    load_y(t).wait()
+                    out[s] = dot(full_v[...], yb[s], TN).astype(BF)
+                else:
+                    out[s] = dot(xb[s], full_v[...], TN).astype(BF)
+                write(t, i).start()
+                serve(PLAN2, 3, t, i)
             return carry
 
         lax.fori_loop(0, TILES, unit, 0)
         for t in (TILES - 2, TILES - 1):
-            for d in writes(t):
-                d.wait()
+            for i in range(3):
+                write(t, i).wait()
 
     pl.run_scoped(weights_phase, bf(ROWS, H), bf(ROWS, H), bf(ROWS, H), bf(2, ROWS, TILE), bf(2, ROWS, TILE),
                   bf(2, TILE, H), bf(2, TILE, H), bf(2, H, TILE), dma(3), dma(2), dma(2), dma(2, 3))
 
-    for c in range(CHUNKS):
-        stage7(c)
+    run(PLAN3)
     for j in range(3):
+        for c in range(CHUNKS):
+            dd(c, j).wait_recv()
         p1(CHUNKS - 1, j).wait_send()
         for c in (CHUNKS - 2, CHUNKS - 1):
             p2(c, j).wait_send()
@@ -361,6 +334,11 @@
             a2(c, j).wait_send()
             a3(c, j).wait_send()
             dd(c, j).wait_send()
+
+
+def hand_over(*refs):
+    for src, dst in zip(refs[:4], refs[4:]):
+        dst[...] = src[...]
 
 
 def solution(mesh):
@@ -382,7 +360,17 @@
             scratch_shapes=scratch,
             compiler_params=pltpu.CompilerParams(collective_id=0, has_side_effects=True, vmem_limit_bytes=67043328),
         )(x, dy, gate, up, w_gate, w_up, w_down)
-        return tuple(res[:4])
+        n = 8
+        specs = [pl.BlockSpec((ROWS // n, D), lambda i: (i, 0)), pl.BlockSpec((D // n, H), lambda i: (i, 0)),
+                 pl.BlockSpec((D // n, H), lambda i: (i, 0)), pl.BlockSpec((H // n, D), lambda i: (i, 0))]
+        return pl.pallas_call(
+            hand_over,
+            grid=(n,),
+            in_specs=specs,
+            out_specs=specs,
+            out_shape=[jax.ShapeDtypeStruct(s, BF) for s in outs[:4]],
+            compiler_params=pltpu.CompilerParams(vmem_limit_bytes=60 << 20),
+        )(*res[:4])
 
     tokens, columns, rows = P("dp", None), P(None, "tp"), P("tp", None)
     return jax.shard_map(

time: 241 us -> 212 us (0.88)
  local copies, waits for them, and re-layouts: 44.7 us -> 0 us
  Pallas kernels: 196 us -> 211 us
    unnamed x4 -> x0, local copies, waits for them, and re-layouts: 44.7 us -> none
    pallas_call x0 -> x1, Pallas kernels: none -> 33.3 us  [step(): pl.pallas_call(hand_over, grid=(n,), in_specs=specs, out_specs=specs, out...]
    pallas_call x1, Pallas kernels: 196 us -> 178 us  [step(): pl.pallas_call(kernel, in_specs=[pl.BlockSpec(memory_space=pl.ANY)] * 7,...]
where the time goes in v2:
time: 212 us
  Pallas kernels  211 us (100%)
    pallas_call x1, Pallas kernels, step(): pl.pallas_call(kernel, in_specs=[pl.BlockSpec(memory_space=pl.ANY)] * 7,...  178 us
    pallas_call x1, Pallas kernels, step(): pl.pallas_call(hand_over, grid=(n,), in_specs=specs, out_specs=specs, out...  33.3 us

profile of v2, /device:TPU:0, one launch (start us, length us, event | category | flops | bytes accessed | tf_op | source)
XLA Modules:
  0.0 211.8 jit_solution(4298268364335000457)
XLA Ops:
  0.6 177.9 %shard_map.102 = (bf16[2048,5120]{1,0:T(8,128)(2,1)}, bf16[5120,1024]{1,0:T(8,128)(2,1)}, bf16[5120,1024]{1,0:T(8,128)(2,1)}, bf16[1024,5120]{1,0:T(8,128)(2,1)}...) custom-call(bf16[2048,5120]{1,0:T(8,128)(2,1)} %x.1, bf16[2048,5120]{1,0:T(8,128)(2,1)} %dy.1, ...), custom_call_target="tpu_custom_call" | custom-call | tf_op jit(solution)/shard_map/pallas_call | solution.py:355
  178.5 33.3 %shard_map.103 = (bf16[2048,5120]{1,0:T(8,128)(2,1)}, bf16[5120,1024]{1,0:T(8,128)(2,1)}, bf16[5120,1024]{1,0:T(8,128)(2,1)}, bf16[1024,5120]{1,0:T(8,128)(2,1)}) custom-call(bf16[2048,5120]{1,0:T(8,128)(2,1)} %get-tuple-element.8.refs_0_, bf16[5120,1024]{1,0:T(8,128)(2,1)} %get-tuple-element.9.refs_1_, bf16[5120,1024]{1,0:T(8,128)(2,1)} %get-tuple-element.10.refs_2_, ...), custom_call_target="tpu_custom_call" | custom-call | tf_op jit(solution)/shard_map/pallas_call | solution.py:366

commit v3 on v2

--- a/solution.py
+++ b/solution.py
@@ -20,12 +20,12 @@
 TILE = 512
 TILES = D // TILE
 
-PLAN1 = {12: [100, 101, 102], 16: [200, 201, 202], 20: [110, 111, 112], 21: [300, 302], 24: [210, 212], 25: [301, 211], 27: [400], 28: [120, 122,
-         121], 30: [310]}
-PLAN2 = {0: [311, 221, 220], 2: [312, 222, 401, 130, 402], 3: [132], 4: [131], 5: [321], 6: [320, 322, 410, 412], 7: [411], 8: [230, 231, 232], 9:
-         [420, 422], 10: [421], 11: [331, 501], 12: [330, 500], 13: [502], 15: [332], 16: [430, 431, 510], 18: [511, 512, 601], 19: [600, 602], 20:
-         [432], 22: [520, 522], 23: [521, 610], 25: [611, 612], 26: [530, 532], 27: [531], 29: [620, 622]}
-PLAN3 = [621, 632, 630, 631]
+PLAN1 = {15: [100], 16: [102, 101], 19: [200], 20: [202], 23: [201], 25: [111, 112, 110], 26: [300], 27: [301, 302], 32: [211], 33: [210, 212], 34:
+         [400, 401], 35: [120, 122, 121], 36: [310, 311], 38: [312, 402], 39: [222]}
+PLAN2 = {1: [220], 2: [221, 501, 131], 3: [130], 4: [322, 321, 411, 500], 5: [410, 320], 6: [231, 132, 230], 9: [422, 412, 502], 10: [331], 11: [420,
+         232], 12: [421], 13: [330, 511], 14: [332], 15: [510, 431], 16: [522], 17: [520, 432, 430], 18: [602], 20: [521, 600], 21: [512, 622], 22:
+         [531], 23: [530, 532], 24: [611], 25: [601, 610], 26: [612], 27: [620], 29: [621]}
+PLAN3 = [632, 631, 630]
 
 
 def dot(a, b, dims):
@@ -35,12 +35,12 @@
 def kernel(x, dy, gate, up, w_gate, w_up, w_down, dx, dwg, dwu, dwd, dg_o, du_o, hd_o,
            acc1, acc2, acc3, ds_, dr, s1, r1, s2, r2, s3, r3, fin,
            d_s, d_r, p1_s, p1_r, p2_s, p2_r, p3_s, p3_r, loc_s,
-           a1_s, a1_r, a2_s, a2_r, a3_s, a3_r, dd_s, dd_r):
+           a1_s, a1_r, a2_s, a2_r, a3_s, a3_r, dd_s, dd_r, de_s, de_r):
     me, dp = lax.axis_index("tp"), lax.axis_index("dp")
     core, bz, by, bx = me % 2, me // 2 % 2, me // 4 % 2, me // 8 % 2
     other = me + 1 - 2 * core
     axes = {"x": (bx, me + 8 - 16 * bx), "y": (by, me + 4 - 8 * by), "z": (bz, me + 2 - 4 * bz)}
-    orders = [[axes[a] for a in o] for o in ("xyz", "yzx", "zxy")]
+    orders = [[axes[a] for a in o] for o in ("yzx", "xyz", "zxy")]
 
     barrier = pltpu.get_barrier_semaphore()
     for peer in (other, axes["x"][1], axes["y"][1], axes["z"][1]):
@@ -82,9 +82,6 @@
     def rows1(c, j):
         return pl.ds(al(base(c) + Q1 * orders[j][0][0], Q1), Q1)
 
-    def rows0(c):
-        return pl.ds(al(base(c), HALF), HALF)
-
     def loc(c, j):
         return pltpu.make_async_copy(fin.at[c % 2, :, cols(j)], dx.at[rows3(c, j), cols(j)], loc_s.at[c % 2, j])
 
@@ -100,8 +97,12 @@
         return remote(r, r, a3_s.at[c, j], a3_r.at[c, j], orders[j][0][1])
 
     def dd(c, j):
-        r = dx.at[rows0(c), cols(j)]
+        r = dx.at[rows1(c, j), cols(j)]
         return remote(r, r, dd_s.at[c, j], dd_r.at[c, j], other)
+
+    def de(c, j):
+        r = dx.at[pl.ds(al(base(c) + Q1 - Q1 * orders[j][0][0], Q1), Q1), cols(j)]
+        return remote(r, r, de_s.at[c, j], de_r.at[c, j], other)
 
     def stage1(c, j):
         bit = orders[j][1][0]
@@ -139,10 +140,11 @@
     def stage5(c, j):
         a2(c, j).wait_recv()
         a3(c, j).start()
+        dd(c, j).start()
 
     def stage6(c, j):
         a3(c, j).wait_recv()
-        dd(c, j).start()
+        de(c, j).start()
 
     stages = (None, stage1, stage2, stage3, stage4, stage5, stage6)
 
@@ -205,6 +207,8 @@
                 dh = dot(dyb[h], wd[part, :], NT)
                 dub[h, :, part] = (dh * silu).astype(BF)
                 dgb[h, :, part] = (dh * u * (sig + silu * (1 - sig))).astype(BF)
+                if i == 0:
+                    serve(PLAN1, 10, c, 5 * h)
             for d in writes(c, h):
                 d.start()
 
@@ -218,7 +222,7 @@
 
         def chunk(c, carry):
             hidden_rows(c, 0)
-            serve(PLAN1, 8, c, 0)
+            serve(PLAN1, 10, c, 1)
             for j in range(3):
                 @pl.when(c == 0)
                 def _():
@@ -230,9 +234,9 @@
                     d_copy(c - 1, j).wait_send()
                 ds_[:, cols(j)] = term(0, j).astype(BF)
                 d_copy(c, j).start()
-                serve(PLAN1, 8, c, 1 + j)
+                serve(PLAN1, 10, c, 2 + j)
             hidden_rows(c, 1)
-            serve(PLAN1, 8, c, 4)
+            serve(PLAN1, 10, c, 6)
             for j in range(3):
                 d_copy(c, j).wait_recv()
 
@@ -244,7 +248,7 @@
                 s1[:, cols(j)] = jnp.where(high, t[:Q1], t[Q1:]).astype(BF)
                 p1(c, j).start()
                 acc1[:, cols(j)] = jnp.where(high, t[Q1:], t[:Q1])
-                serve(PLAN1, 8, c, 5 + j)
+                serve(PLAN1, 10, c, 7 + j)
             return carry
 
         lax.fori_loop(0, CHUNKS, chunk, 0)
@@ -325,6 +329,7 @@
     for j in range(3):
         for c in range(CHUNKS):
             dd(c, j).wait_recv()
+            de(c, j).wait_recv()
         p1(CHUNKS - 1, j).wait_send()
         for c in (CHUNKS - 2, CHUNKS - 1):
             p2(c, j).wait_send()
@@ -334,6 +339,7 @@
             a2(c, j).wait_send()
             a3(c, j).wait_send()
             dd(c, j).wait_send()
+            de(c, j).wait_send()
 
 
 def hand_over(*refs):
@@ -351,7 +357,7 @@
                    bf(HALF, D), bf(2, HALF, D), bf(Q1, D), bf(2, Q1, D), bf(2, Q2, D), bf(2, Q2, D),
                    bf(2, Q3, D), bf(2, Q3, D), bf(2, Q3, D),
                    dma(3), dma(2, 3), dma(3), dma(2, 3), dma(2, 3), dma(2, 3), dma(2, 3), dma(2, 3), dma(2, 3)]
-        scratch += [dma(CHUNKS, 3)] * 8
+        scratch += [dma(CHUNKS, 3)] * 10
         res = pl.pallas_call(
             kernel,
             in_specs=[pl.BlockSpec(memory_space=pl.ANY)] * 7,

time: 212 us -> 209 us (0.986)
  Pallas kernels: 211 us -> 208 us
    pallas_call x1, Pallas kernels: 178 us -> 175 us  [step(): pl.pallas_call(kernel, in_specs=[pl.BlockSpec(memory_space=pl.ANY)] * 7,...]
where the time goes in v3:
time: 209 us
  Pallas kernels  208 us (100%)
    pallas_call x1, Pallas kernels, step(): pl.pallas_call(kernel, in_specs=[pl.BlockSpec(memory_space=pl.ANY)] * 7,...  175 us
    pallas_call x1, Pallas kernels, step(): pl.pallas_call(hand_over, grid=(n,), in_specs=specs, out_specs=specs, out...  33.3 us

profile of v3, /device:TPU:0, one launch (start us, length us, event | category | flops | bytes accessed | tf_op | source)
XLA Modules:
  0.0 208.7 jit_solution(5341464408739520492)
XLA Ops:
  0.6 174.7 %shard_map.102 = (bf16[2048,5120]{1,0:T(8,128)(2,1)}, bf16[5120,1024]{1,0:T(8,128)(2,1)}, bf16[5120,1024]{1,0:T(8,128)(2,1)}, bf16[1024,5120]{1,0:T(8,128)(2,1)}...) custom-call(bf16[2048,5120]{1,0:T(8,128)(2,1)} %x.1, bf16[2048,5120]{1,0:T(8,128)(2,1)} %dy.1, ...), custom_call_target="tpu_custom_call" | custom-call | tf_op jit(solution)/shard_map/pallas_call | solution.py:361
  175.4 33.3 %shard_map.103 = (bf16[2048,5120]{1,0:T(8,128)(2,1)}, bf16[5120,1024]{1,0:T(8,128)(2,1)}, bf16[5120,1024]{1,0:T(8,128)(2,1)}, bf16[1024,5120]{1,0:T(8,128)(2,1)}) custom-call(bf16[2048,5120]{1,0:T(8,128)(2,1)} %get-tuple-element.8.refs_0_, bf16[5120,1024]{1,0:T(8,128)(2,1)} %get-tuple-element.9.refs_1_, bf16[5120,1024]{1,0:T(8,128)(2,1)} %get-tuple-element.10.refs_2_, ...), custom_call_target="tpu_custom_call" | custom-call | tf_op jit(solution)/shard_map/pallas_call | solution.py:372

commit v4 on v3

--- a/solution.py
+++ b/solution.py
@@ -17,6 +17,7 @@
 HALF = ROWS // CHUNKS // 2
 Q1, Q2, Q3 = HALF // 2, HALF // 4, HALF // 8
 COLS = ((0, 1792), (1792, 1792), (3584, 1536))
+LAST = 256
 TILE = 512
 TILES = D // TILE
 
@@ -217,8 +218,12 @@
                 for d in loads(c + 1, h):
                     d.start()
 
-        def term(h, j):
-            return dot(dgb[h], wg[cols(j), :], NT) + dot(dub[h], wu[cols(j), :], NT)
+        def term(h, at):
+            return dot(dgb[h], wg[at, :], NT) + dot(dub[h], wu[at, :], NT)
+
+        def pieces(j):
+            start, width = COLS[j]
+            return [pl.ds(start, width - LAST), pl.ds(start + width - LAST, LAST)]
 
         def chunk(c, carry):
             hidden_rows(c, 0)
@@ -232,7 +237,8 @@
                 @pl.when(c >= 1)
                 def _():
                     d_copy(c - 1, j).wait_send()
-                ds_[:, cols(j)] = term(0, j).astype(BF)
+                for at in pieces(j):
+                    ds_[:, at] = term(0, at).astype(BF)
                 d_copy(c, j).start()
                 serve(PLAN1, 10, c, 2 + j)
             hidden_rows(c, 1)
@@ -243,11 +249,12 @@
                 @pl.when(c >= 1)
                 def _():
                     p1(c - 1, j).wait_send()
-                t = term(1, j) + dr[c % 2, :, cols(j)].astype(F32)
                 high = orders[j][0][0] == 1
-                s1[:, cols(j)] = jnp.where(high, t[:Q1], t[Q1:]).astype(BF)
+                for at in pieces(j):
+                    t = term(1, at) + dr[c % 2, :, at].astype(F32)
+                    s1[:, at] = jnp.where(high, t[:Q1], t[Q1:]).astype(BF)
+                    acc1[:, at] = jnp.where(high, t[Q1:], t[:Q1])
                 p1(c, j).start()
-                acc1[:, cols(j)] = jnp.where(high, t[Q1:], t[:Q1])
                 serve(PLAN1, 10, c, 7 + j)
             return carry
 

time: 209 us -> 208 us (level)
  no operation moved by 1% of the time
where the time goes in v4:
time: 208 us
  Pallas kernels  207 us (100%)
    pallas_call x1, Pallas kernels, step(): pl.pallas_call(kernel, in_specs=[pl.BlockSpec(memory_space=pl.ANY)] * 7,...  174 us
    pallas_call x1, Pallas kernels, step(): pl.pallas_call(hand_over, grid=(n,), in_specs=specs, out_specs=specs, out...  33.3 us

profile of v4, /device:TPU:0, one launch (start us, length us, event | category | flops | bytes accessed | tf_op | source)
XLA Modules:
  0.0 207.7 jit_solution(11497475864355608584)
XLA Ops:
  0.6 173.7 %shard_map.102 = (bf16[2048,5120]{1,0:T(8,128)(2,1)}, bf16[5120,1024]{1,0:T(8,128)(2,1)}, bf16[5120,1024]{1,0:T(8,128)(2,1)}, bf16[1024,5120]{1,0:T(8,128)(2,1)}...) custom-call(bf16[2048,5120]{1,0:T(8,128)(2,1)} %x.1, bf16[2048,5120]{1,0:T(8,128)(2,1)} %dy.1, ...), custom_call_target="tpu_custom_call" | custom-call | tf_op jit(solution)/shard_map/pallas_call | solution.py:368
  174.3 33.3 %shard_map.103 = (bf16[2048,5120]{1,0:T(8,128)(2,1)}, bf16[5120,1024]{1,0:T(8,128)(2,1)}, bf16[5120,1024]{1,0:T(8,128)(2,1)}, bf16[1024,5120]{1,0:T(8,128)(2,1)}) custom-call(bf16[2048,5120]{1,0:T(8,128)(2,1)} %get-tuple-element.8.refs_0_, bf16[5120,1024]{1,0:T(8,128)(2,1)} %get-tuple-element.9.refs_1_, bf16[5120,1024]{1,0:T(8,128)(2,1)} %get-tuple-element.10.refs_2_, ...), custom_call_target="tpu_custom_call" | custom-call | tf_op jit(solution)/shard_map/pallas_call | solution.py:379

commit v5 on v4

--- a/solution.py
+++ b/solution.py
@@ -223,7 +223,7 @@
 
         def pieces(j):
             start, width = COLS[j]
-            return [pl.ds(start, width - LAST), pl.ds(start + width - LAST, LAST)]
+            return [pl.ds(start, 768), pl.ds(start + 768, width - LAST - 768), pl.ds(start + width - LAST, LAST)]
 
         def chunk(c, carry):
             hidden_rows(c, 0)

time: 208 us -> 208 us (level)
  no operation moved by 1% of the time
where the time goes in v5:
time: 208 us; the launch traced here: 207 us
  Pallas kernels  207 us (100%)
    pallas_call x1, Pallas kernels, step(): pl.pallas_call(kernel, in_specs=[pl.BlockSpec(memory_space=pl.ANY)] * 7,...  173 us
    pallas_call x1, Pallas kernels, step(): pl.pallas_call(hand_over, grid=(n,), in_specs=specs, out_specs=specs, out...  33.3 us

profile of v5, /device:TPU:0, one launch (start us, length us, event | category | flops | bytes accessed | tf_op | source)
XLA Modules:
  0.0 207.4 jit_solution(13467360316644016025)
XLA Ops:
  0.6 173.4 %shard_map.102 = (bf16[2048,5120]{1,0:T(8,128)(2,1)}, bf16[5120,1024]{1,0:T(8,128)(2,1)}, bf16[5120,1024]{1,0:T(8,128)(2,1)}, bf16[1024,5120]{1,0:T(8,128)(2,1)}...) custom-call(bf16[2048,5120]{1,0:T(8,128)(2,1)} %x.1, bf16[2048,5120]{1,0:T(8,128)(2,1)} %dy.1, ...), custom_call_target="tpu_custom_call" | custom-call | tf_op jit(solution)/shard_map/pallas_call | solution.py:368
  174.1 33.3 %shard_map.103 = (bf16[2048,5120]{1,0:T(8,128)(2,1)}, bf16[5120,1024]{1,0:T(8,128)(2,1)}, bf16[5120,1024]{1,0:T(8,128)(2,1)}, bf16[1024,5120]{1,0:T(8,128)(2,1)}) custom-call(bf16[2048,5120]{1,0:T(8,128)(2,1)} %get-tuple-element.8.refs_0_, bf16[5120,1024]{1,0:T(8,128)(2,1)} %get-tuple-element.9.refs_1_, bf16[5120,1024]{1,0:T(8,128)(2,1)} %get-tuple-element.10.refs_2_, ...), custom_call_target="tpu_custom_call" | custom-call | tf_op jit(solution)/shard_map/pallas_call | solution.py:379
